TPU v7x, 32 devices: a whole 2x2x4 slice. The times are simulated.
32 devices in a mesh: cut: 8 (over z, y), sub: 4 (over x, core).
Axes of the slice: x: 2, y: 2, z: 4, core: 2. Of those that a mesh axis runs over, the one named last changes fastest.
Arguments:
- residual: bfloat16 [8, 4, 1024, 128], P('cut', 'sub'), may hold values from -6 to 6
- inner_inverse: bfloat16 [8, 4, 4, 343, 343], P('cut', 'sub'), may hold values from -0.3125 to 0.3125
- inner_index: int32 [8, 4, 4, 343], P('cut', 'sub'), may hold values from 0 to 1023
- slab_dofs: int32 [8, 4, 5, 512], P('cut', 'sub'), may hold values from 0 to 1023
- face_inverse: bfloat16 [8, 4, 5, 3, 343, 343], P('cut', 'sub'), may hold values from -0.3125 to 0.3125
- face_index: int32 [8, 4, 5, 3, 343], P('cut', 'sub'), may hold values from 0 to 1023
- face_count: int32 [8, 4, 5], P('cut', 'sub'), may hold values from 1 to 3
Outputs:
- correction: float32 [8, 4, 1024, 128], P('cut', 'sub')
All inputs are finite; a program needn't handle non-finite values.
Results may differ from a plain program's by a relative error of at most 0.0003.
Values may be sent and summed in bfloat16 or wider, within the bound.
A program may use at most 64 MiB of HBM per device.

v0:
```python
import jax
import jax.numpy as jnp
from jax import lax
from jax.experimental import pallas as pl
from jax.experimental.pallas import tpu as pltpu
from jax.sharding import PartitionSpec as P

CUTLV = 3
LANES = 128
CHUNK = 128
MESH = pl.DeviceIdType.MESH


def round_up(value, step):
    return (value + step - 1) // step * step


def split_pair(values):
    high = values.astype(jnp.bfloat16)
    low = (values - high.astype(jnp.float32)).astype(jnp.bfloat16)
    return high, low


def make_kernel(ndof, nrhs, nint, star, levels, slots, slab, order):
    pad = round_up(star, LANES)
    joint = 2 * slab

    def kernel(
        res, inner_inv, inner_idx, dofs, face_inv, face_idx, counts, out,
        inv_in, inv_face, rows, row_t, dof_t,
        pick, s_in, st_in, s_face, st_face, p_t,
        gathered, pair, joined, terms, back, acc,
        inv_sem, send_sem, recv_sem, give_sem, back_sem,
    ):
        copies = [pltpu.make_async_copy(inner_inv.at[0, 0], inv_in, inv_sem.at[levels])]
        for k in range(levels):
            copies.append(
                pltpu.make_async_copy(face_inv.at[0, 0, k], inv_face.at[k], inv_sem.at[k])
            )
        for copy in copies:
            copy.start()

        places = []
        for k in range(levels):
            axis = "cut" if k < CUTLV else "sub"
            bits = lax.axis_size(axis).bit_length() - 1
            apart = bits - 1 - (k if k < CUTLV else k - CUTLV)
            me = lax.axis_index(axis)
            upper = lax.rem(lax.div(me, 1 << apart), 2)
            far = me + (1 - 2 * upper) * (1 << apart)
            own_at = pl.multiple_of(upper * slab, slab)
            far_at = pl.multiple_of((1 - upper) * slab, slab)
            places.append(({axis: far}, own_at, far_at))

        barrier = pltpu.get_barrier_semaphore()
        for target, _, _ in places:
            pl.semaphore_signal(barrier, inc=1, device_id=target, device_id_type=MESH)

        rows[...] = jnp.full(rows.shape, -1, jnp.int32)
        rows[0:nint, 0:star] = inner_idx[0, 0]
        for k in range(levels):
            for j in range(slots):
                at = nint + k * slots + j
                live = j < counts[0, 0, k]
                rows[at : at + 1, 0:star] = jnp.where(live, face_idx[0, 0, k, j : j + 1], -1)
        row_t[...] = rows[...].T
        dof_rows = jnp.concatenate(
            [dofs[0, 0], jnp.full((round_up(levels, 8) - levels, slab), -1, jnp.int32)], axis=0
        )
        dof_t[...] = dof_rows.T

        def across(column, width):
            spots = lax.broadcasted_iota(jnp.int32, (column.shape[0], width), 1)
            return jnp.where(column == spots, 1.0, 0.0).astype(jnp.bfloat16)

        def down(row, first, height):
            spots = lax.broadcasted_iota(jnp.int32, (height, row.shape[1]), 0) + first
            return jnp.where(row == spots, 1.0, 0.0).astype(jnp.bfloat16)

        send, give = [], []
        for k, (target, own_at, far_at) in enumerate(places):
            send.append(
                pltpu.make_async_remote_copy(
                    src_ref=joined.at[k, pl.ds(own_at, slab)],
                    dst_ref=joined.at[k, pl.ds(own_at, slab)],
                    send_sem=send_sem.at[k],
                    recv_sem=recv_sem.at[k],
                    device_id=target,
                    device_id_type=MESH,
                )
            )
            give.append(
                pltpu.make_async_remote_copy(
                    src_ref=terms.at[k, pl.ds(far_at, slab)],
                    dst_ref=back.at[k],
                    send_sem=give_sem.at[k],
                    recv_sem=back_sem.at[k],
                    device_id=target,
                    device_id_type=MESH,
                )
            )

        for k, (_, own_at, _) in enumerate(places):
            for first in range(0, slab, CHUNK):
                pick[first : first + CHUNK] = across(dof_t[first : first + CHUNK, k : k + 1], ndof)
            mine = jnp.dot(pick[...], res[0, 0], preferred_element_type=jnp.float32)
            joined[k, pl.ds(own_at, slab)] = mine.astype(jnp.bfloat16)
            if k == 1:
                pl.semaphore_wait(barrier, levels)
            if k >= 1:
                send[k - 1].start()

        def build_down(target, row_of, count, height):
            def step(i, carry):
                first = pl.multiple_of(i * CHUNK, CHUNK)
                for j in range(count):
                    row = rows[row_of + j : row_of + j + 1, :]
                    target[pl.ds(first, CHUNK), j * pad : (j + 1) * pad] = down(row, first, CHUNK)
                return carry

            lax.fori_loop(0, height // CHUNK, step, 0)

        def build_across(target, row_of, count, width):
            for j in range(count):
                for first in range(0, pad, CHUNK):
                    column = row_t[first : first + CHUNK, row_of + j : row_of + j + 1]
                    target[j * pad + first : j * pad + first + CHUNK, :] = across(column, width)

        build_across(s_in, 0, nint, ndof)
        send[levels - 1].start()
        build_down(st_in, 0, nint, ndof)

        def solve(selector, source, inverses, count):
            gathered[0 : count * pad] = jnp.dot(
                selector, source, preferred_element_type=jnp.float32
            ).astype(jnp.bfloat16)
            for j in range(count):
                solved = jnp.dot(
                    inverses[j],
                    gathered[j * pad : j * pad + star],
                    preferred_element_type=jnp.float32,
                )
                high, low = split_pair(solved)
                pair[j * pad : j * pad + star, 0:nrhs] = high
                pair[j * pad : j * pad + star, nrhs : 2 * nrhs] = low

        pair[...] = jnp.zeros(pair.shape, jnp.bfloat16)
        copies[0].wait()
        solve(s_in[...], res[0, 0], inv_in, nint)
        acc[...] = jnp.dot(
            st_in[...], pair[0 : nint * pad], preferred_element_type=jnp.float32
        )

        for k in order:
            build_across(s_face.at[k], nint + k * slots, slots, joint)
            build_down(st_face.at[k], nint + k * slots, slots, joint)

        for k in range(levels):
            def step(i, carry):
                first = pl.multiple_of(i * CHUNK, CHUNK)
                p_t[k, pl.ds(first, CHUNK), :] = down(dofs[0, 0, k : k + 1, :], first, CHUNK)
                return carry

            lax.fori_loop(0, ndof // CHUNK, step, 0)

        for k in order:
            _, own_at, far_at = places[k]
            send[k].wait_recv()
            copies[1 + k].wait()
            solve(s_face[k], joined[k], inv_face.at[k], slots)
            for at in (far_at, own_at):
                both = jnp.dot(
                    st_face[k, pl.ds(at, slab), :],
                    pair[0 : slots * pad],
                    preferred_element_type=jnp.float32,
                )
                terms[k, pl.ds(at, slab), :] = both[:, :nrhs] + both[:, nrhs:]
            give[k].start()

        for k in order:
            _, own_at, _ = places[k]
            give[k].wait_recv()
            high, low = split_pair(terms[k, pl.ds(own_at, slab), :] + back[k])
            pair[0:slab, 0:nrhs] = high
            pair[0:slab, nrhs : 2 * nrhs] = low
            acc[...] += jnp.dot(p_t[k], pair[0:slab], preferred_element_type=jnp.float32)
        out[0, 0] = acc[:, :nrhs] + acc[:, nrhs:]
        for k in range(levels):
            send[k].wait_send()
            give[k].wait_send()

    return kernel


def on_device(
    residual, inner_inverse, inner_index, slab_dofs, face_inverse, face_index, face_count
):
    ndof, nrhs = residual.shape[2:]
    nint, star = inner_index.shape[2:]
    levels, slots = face_index.shape[2:4]
    slab = slab_dofs.shape[3]
    pad = round_up(star, LANES)
    joint = 2 * slab
    index_rows = round_up(nint + levels * slots, 8)
    order = (4, 3, 2, 0, 1)
    kinds = jnp.bfloat16
    vmem = pl.BlockSpec(memory_space=pltpu.VMEM)
    anywhere = pl.BlockSpec(memory_space=pl.ANY)
    scalar = pl.BlockSpec(memory_space=pltpu.SMEM)
    return pl.pallas_call(
        make_kernel(ndof, nrhs, nint, star, levels, slots, slab, order),
        out_shape=jax.ShapeDtypeStruct(residual.shape, jnp.float32),
        in_specs=[vmem, anywhere, vmem, vmem, anywhere, vmem, scalar],
        out_specs=vmem,
        scratch_shapes=[
            pltpu.VMEM((nint, star, star), kinds),
            pltpu.VMEM((levels, slots, star, star), kinds),
            pltpu.VMEM((index_rows, pad), jnp.int32),
            pltpu.VMEM((pad, index_rows), jnp.int32),
            pltpu.VMEM((slab, round_up(levels, 8)), jnp.int32),
            pltpu.VMEM((slab, ndof), kinds),
            pltpu.VMEM((nint * pad, ndof), kinds),
            pltpu.VMEM((ndof, nint * pad), kinds),
            pltpu.VMEM((levels, slots * pad, joint), kinds),
            pltpu.VMEM((levels, joint, slots * pad), kinds),
            pltpu.VMEM((levels, ndof, slab), kinds),
            pltpu.VMEM((max(nint, slots) * pad, nrhs), kinds),
            pltpu.VMEM((max(nint, slots) * pad, 2 * nrhs), kinds),
            pltpu.VMEM((levels, joint, nrhs), kinds),
            pltpu.VMEM((levels, joint, nrhs), jnp.float32),
            pltpu.VMEM((levels, slab, nrhs), jnp.float32),
            pltpu.VMEM((ndof, 2 * nrhs), jnp.float32),
            pltpu.SemaphoreType.DMA((levels + 1,)),
            pltpu.SemaphoreType.DMA((levels,)),
            pltpu.SemaphoreType.DMA((levels,)),
            pltpu.SemaphoreType.DMA((levels,)),
            pltpu.SemaphoreType.DMA((levels,)),
        ],
        compiler_params=pltpu.CompilerParams(
            collective_id=0, has_side_effects=True, vmem_limit_bytes=64000000
        ),
    )(residual, inner_inverse, inner_index, slab_dofs, face_inverse, face_index, face_count)


def solution(mesh):
    return jax.shard_map(
        on_device,
        mesh=mesh,
        in_specs=(
            P("cut", "sub", None, None),
            P("cut", "sub", None, None, None),
            P("cut", "sub", None, None),
            P("cut", "sub", None, None),
            P("cut", "sub", None, None, None, None),
            P("cut", "sub", None, None, None),
            P("cut", "sub", None),
        ),
        out_specs=P("cut", "sub", None, None),
        check_vma=False,
    )
```

profile of v0, /device:TPU:0, one launch (start us, length us, event | category | flops | bytes accessed | tf_op | source)
XLA Modules:
  0.0 52.2 jit_solution(5617555280814895389)
XLA Ops:
  0.0 1.3 %copy.9.dofs = s32[1,1,5,512]{3,2,1,0:T(8,128)} copy(s32[1,1,5,512]{3,1,2,0:T(1,128)} %param.10) | data formatting | bytes 20480 | tf_op args[3]
  1.3 1.4 %copy.10.face_idx = s32[1,1,5,3,343]{4,3,2,1,0:T(4,128)} copy(s32[1,1,5,3,343]{4,1,3,2,0:T(1,128)} %param.12) | data formatting | bytes 41160 | tf_op args[5]
  2.7 2.4 %copy.8.inner_inv = bf16[1,1,4,343,343]{4,3,2,1,0:T(8,128)(2,1)} copy(bf16[1,1,4,343,343]{4,2,3,1,0:T(4,128)(2,1)} %param.8) | data formatting | bytes 1882384 | tf_op args[1]
  5.0 45.3 %shard_map.73 = f32[1,1,1024,128]{3,2,1,0:T(8,128)} custom-call(bf16[1,1,1024,128]{3,2,1,0:T(8,128)(2,1)} %res.1, bf16[1,1,4,343,343]{4,3,2,1,0:T(8,128)(2,1)} %copy.8.inner_inv, s32[1,1,4,343]{3,2,1,0:T(4,128)} %inner_idx.1, s32[1,1,5,512]{3,2,1,0:T(8,128)} %copy.9.dofs, bf16[1,1,5,3,343,343]{5,4,3,2,1,0:T(8,128)(2,1)} %face_inv.1, ...), custom_call_target="tpu_custom_call" | custom-call | tf_op jit(solution)/shard_map/pallas_call | solution.py:210
  50.3 1.9 %copy.12 = f32[1,1,1024,128]{3,2,1,0:T(8,128)} copy(f32[1,1,1024,128]{3,2,1,0:T(8,128)} %shard_map.73) | data formatting | bytes 1048576
where the time goes:
time: 52.5 us; the launch traced here: 52.2 us
  Pallas kernels  45.3 us (86%)
  local copies, waits for them, and re-layouts  6.87 us (13%)
    pallas_call x1, Pallas kernels, on_device(): pl.pallas_call(make_kernel(ndof, nrhs, nint, star, levels, slots, slab, o...  45.3 us
    unnamed x4, local copies, waits for them, and re-layouts  6.87 us

commit v1 on v0

v1 whole, which is shorter than its diff:
```python
import jax
import jax.numpy as jnp
from jax import lax
from jax.experimental import pallas as pl
from jax.experimental.pallas import tpu as pltpu
from jax.sharding import PartitionSpec as P

CUTLV = 3
LANES = 128
CHUNK = 128
INDEX = jnp.int16
MESH = pl.DeviceIdType.MESH


def round_up(value, step):
    return (value + step - 1) // step * step


def split_pair(values):
    high = values.astype(jnp.bfloat16)
    low = (values - high.astype(jnp.float32)).astype(jnp.bfloat16)
    return high, low


def make_kernel(ndof, nrhs, nint, star, levels, slots, slab, early, order, finish):
    pad = round_up(star, LANES)
    joint = 2 * slab

    def kernel(
        res, inner_inv, inner_idx, dofs, face_inv, face_idx, counts, out,
        inv_in, inv_face, rows, res_t, st_in, st_face, p_t,
        gathered, pair, joined, terms, back, acc,
        inv_sem, send_sem, recv_sem, give_sem, back_sem,
    ):
        copies = [pltpu.make_async_copy(inner_inv.at[0, 0], inv_in, inv_sem.at[levels])]
        for k in range(levels):
            copies.append(
                pltpu.make_async_copy(face_inv.at[0, 0, k], inv_face.at[k], inv_sem.at[k])
            )
        for copy in copies:
            copy.start()

        places = []
        for k in range(levels):
            axis = "cut" if k < CUTLV else "sub"
            bits = lax.axis_size(axis).bit_length() - 1
            apart = bits - 1 - (k if k < CUTLV else k - CUTLV)
            me = lax.axis_index(axis)
            upper = lax.rem(lax.div(me, 1 << apart), 2)
            far = me + (1 - 2 * upper) * (1 << apart)
            places.append(({axis: far}, upper, 1 - upper))

        barrier = pltpu.get_barrier_semaphore()
        for target, _, _ in places:
            pl.semaphore_signal(barrier, inc=1, device_id=target, device_id_type=MESH)

        def down(row, first, height):
            shape = (height, row.shape[1])
            spots = (lax.broadcasted_iota(jnp.int32, shape, 0) + first).astype(INDEX)
            wanted = jnp.broadcast_to(row, shape).astype(INDEX)
            one, zero = jnp.bfloat16(1), jnp.bfloat16(0)
            return jnp.where(wanted == spots, one, zero)

        def build_slab(k):
            def step(i, carry):
                first = pl.multiple_of(i * CHUNK, CHUNK)
                p_t[k, pl.ds(first, CHUNK), :] = down(dofs[k], first, CHUNK)
                return carry

            lax.fori_loop(0, ndof // CHUNK, step, 0)

        def build_stars(target, row_of, count, height):
            def step(i, carry):
                first = pl.multiple_of(i * CHUNK, CHUNK)
                for j in range(count):
                    row = rows[row_of + j : row_of + j + 1, :]
                    target[pl.ds(first, CHUNK), j * pad : (j + 1) * pad] = down(row, first, CHUNK)
                return carry

            lax.fori_loop(0, height // CHUNK, step, 0)

        def build_face(k):
            build_stars(st_face.at[k], nint + k * slots, slots, joint)

        send, give = [], []
        for k, (target, own, far) in enumerate(places):
            send.append(
                pltpu.make_async_remote_copy(
                    src_ref=joined.at[k, own],
                    dst_ref=joined.at[k, own],
                    send_sem=send_sem.at[k],
                    recv_sem=recv_sem.at[k],
                    device_id=target,
                    device_id_type=MESH,
                )
            )
            give.append(
                pltpu.make_async_remote_copy(
                    src_ref=terms.at[k, far],
                    dst_ref=back.at[k],
                    send_sem=give_sem.at[k],
                    recv_sem=back_sem.at[k],
                    device_id=target,
                    device_id_type=MESH,
                )
            )

        res_t[...] = res[0, 0].T
        for k, (_, own, _) in enumerate(places):
            build_slab(k)
            if k == 1:
                pl.semaphore_wait(barrier, levels)
            if k >= 1:
                send[k - 1].start()
            mine = jnp.dot(res_t[...], p_t[k], preferred_element_type=jnp.float32)
            joined[k, own] = mine.astype(jnp.bfloat16)

        rows[...] = jnp.full(rows.shape, -1, jnp.int32)
        rows[0:nint, 0:star] = inner_idx[0, 0]
        for k in range(levels):
            for j in range(slots):
                at = nint + k * slots + j
                live = j < counts[0, 0, k]
                rows[at : at + 1, 0:star] = jnp.where(live, face_idx[k * slots + j], -1)
        pair[...] = jnp.zeros(pair.shape, jnp.bfloat16)
        send[levels - 1].start()

        def solve(picked, inverses, count):
            gathered[:, 0 : count * pad] = picked.astype(jnp.bfloat16)
            for j in range(count):
                solved = lax.dot_general(
                    inverses[j],
                    gathered[:, j * pad : j * pad + star],
                    (((1,), (1,)), ((), ())),
                    preferred_element_type=jnp.float32,
                )
                high, low = split_pair(solved)
                pair[j * pad : j * pad + star, 0:nrhs] = high
                pair[j * pad : j * pad + star, nrhs : 2 * nrhs] = low

        def face(k):
            _, own, far = places[k]
            send[k].wait_recv()
            copies[1 + k].wait()
            picked = jnp.dot(
                joined[k, 0], st_face[k, 0:slab, :], preferred_element_type=jnp.float32
            ) + jnp.dot(
                joined[k, 1], st_face[k, slab:joint, :], preferred_element_type=jnp.float32
            )
            solve(picked, inv_face.at[k], slots)
            for half in (far, own):
                at = pl.multiple_of(half * slab, slab)
                both = jnp.dot(
                    st_face[k, pl.ds(at, slab), :],
                    pair[0 : slots * pad],
                    preferred_element_type=jnp.float32,
                )
                terms[k, half] = both[:, :nrhs] + both[:, nrhs:]
            give[k].start()

        for k in early:
            build_face(k)
        build_stars(st_in, 0, nint, ndof)
        copies[0].wait()
        solve(
            jnp.dot(res_t[...], st_in[...], preferred_element_type=jnp.float32), inv_in, nint
        )
        acc[...] = jnp.dot(
            st_in[...], pair[0 : nint * pad], preferred_element_type=jnp.float32
        )
        for k in order:
            if k not in early:
                build_face(k)
            face(k)

        for k in finish:
            _, own, _ = places[k]
            give[k].wait_recv()
            high, low = split_pair(terms[k, own] + back[k])
            pair[0:slab, 0:nrhs] = high
            pair[0:slab, nrhs : 2 * nrhs] = low
            both = jnp.dot(p_t[k], pair[0:slab], preferred_element_type=jnp.float32)
            if k == finish[-1]:
                both = acc[...] + both
                out[0, 0] = both[:, :nrhs] + both[:, nrhs:]
            else:
                acc[...] += both
        for k in range(levels):
            send[k].wait_send()
            give[k].wait_send()

    return kernel


def on_device(
    residual, inner_inverse, inner_index, slab_dofs, face_inverse, face_index, face_count
):
    ndof, nrhs = residual.shape[2:]
    nint, star = inner_index.shape[2:]
    levels, slots = face_index.shape[2:4]
    slab = slab_dofs.shape[3]
    pad = round_up(star, LANES)
    joint = 2 * slab
    index_rows = round_up(nint + levels * slots, 8)
    early, order, finish = (0, 1, 2), (0, 1, 2, 3, 4), (2, 3, 4, 1, 0)
    kinds = jnp.bfloat16
    vmem = pl.BlockSpec(memory_space=pltpu.VMEM)
    anywhere = pl.BlockSpec(memory_space=pl.ANY)
    scalar = pl.BlockSpec(memory_space=pltpu.SMEM)
    most = max(nint, slots) * pad
    return pl.pallas_call(
        make_kernel(ndof, nrhs, nint, star, levels, slots, slab, early, order, finish),
        out_shape=jax.ShapeDtypeStruct(residual.shape, jnp.float32),
        in_specs=[vmem, anywhere, vmem, vmem, anywhere, vmem, scalar],
        out_specs=vmem,
        scratch_shapes=[
            pltpu.VMEM((nint, star, star), kinds),
            pltpu.VMEM((levels, slots, star, star), kinds),
            pltpu.VMEM((index_rows, pad), jnp.int32),
            pltpu.VMEM((nrhs, ndof), kinds),
            pltpu.VMEM((ndof, nint * pad), kinds),
            pltpu.VMEM((levels, joint, slots * pad), kinds),
            pltpu.VMEM((levels, ndof, slab), kinds),
            pltpu.VMEM((nrhs, most), kinds),
            pltpu.VMEM((max(most, slab), 2 * nrhs), kinds),
            pltpu.VMEM((levels, 2, nrhs, slab), kinds),
            pltpu.VMEM((levels, 2, slab, nrhs), jnp.float32),
            pltpu.VMEM((levels, slab, nrhs), jnp.float32),
            pltpu.VMEM((ndof, 2 * nrhs), jnp.float32),
            pltpu.SemaphoreType.DMA((levels + 1,)),
            pltpu.SemaphoreType.DMA((levels,)),
            pltpu.SemaphoreType.DMA((levels,)),
            pltpu.SemaphoreType.DMA((levels,)),
            pltpu.SemaphoreType.DMA((levels,)),
        ],
        compiler_params=pltpu.CompilerParams(
            collective_id=0, has_side_effects=True, vmem_limit_bytes=64000000
        ),
    )(
        residual,
        inner_inverse,
        inner_index,
        slab_dofs.reshape(levels, 1, slab),
        face_inverse,
        face_index.reshape(levels * slots, 1, star),
        face_count,
    )


def solution(mesh):
    return jax.shard_map(
        on_device,
        mesh=mesh,
        in_specs=(
            P("cut", "sub", None, None),
            P("cut", "sub", None, None, None),
            P("cut", "sub", None, None),
            P("cut", "sub", None, None),
            P("cut", "sub", None, None, None, None),
            P("cut", "sub", None, None, None),
            P("cut", "sub", None),
        ),
        out_specs=P("cut", "sub", None, None),
        check_vma=False,
    )
```

time: 52.5 us -> 34.3 us (0.65)
  Pallas kernels: 45.3 us -> 29.9 us
  local copies, waits for them, and re-layouts: 6.87 us -> 4.22 us
    pallas_call x1, Pallas kernels: 45.3 us -> 29.9 us  [on_device(): pl.pallas_call(make_kernel(ndof, nrhs, nint, star, levels, slots, slab, e...]
    unnamed x4 -> x2, local copies, waits for them, and re-layouts: 6.87 us -> 4.22 us
where the time goes in v1:
time: 34.3 us; the launch traced here: 34.1 us
  Pallas kernels  29.9 us (87%)
  local copies, waits for them, and re-layouts  4.22 us (12%)
    pallas_call x1, Pallas kernels, on_device(): pl.pallas_call(make_kernel(ndof, nrhs, nint, star, levels, slots, slab, e...  29.9 us
    unnamed x2, local copies, waits for them, and re-layouts  4.22 us

profile of v1, /device:TPU:0, one launch (start us, length us, event | category | flops | bytes accessed | tf_op | source)
XLA Modules:
  0.0 34.1 jit_solution(1683837508603932612)
XLA Ops:
  0.0 2.4 %copy.8.inner_inv = bf16[1,1,4,343,343]{4,3,2,1,0:T(8,128)(2,1)} copy(bf16[1,1,4,343,343]{4,2,3,1,0:T(4,128)(2,1)} %param.8) | data formatting | bytes 1882384 | tf_op args[1]
  2.4 29.9 %shard_map.73 = f32[1,1,1024,128]{3,2,1,0:T(8,128)} custom-call(bf16[1,1,1024,128]{3,2,1,0:T(8,128)(2,1)} %res.1, bf16[1,1,4,343,343]{4,3,2,1,0:T(8,128)(2,1)} %copy.8.inner_inv, s32[1,1,4,343]{3,2,1,0:T(4,128)} %inner_idx.1, s32[5,1,512]{2,1,0:T(1,128)} %bitcast.3, bf16[1,1,5,3,343,343]{5,4,3,2,1,0:T(8,128)(2,1)} %face_inv.1, s32[15,1,343]{2,1,0:T(1,128)} %bitcast.2, ...), custom_call_target="tpu_custom_call" | custom-call | tf_op jit(solution)/shard_map/pallas_call | solution.py:211
  32.2 1.9 %copy.10 = f32[1,1,1024,128]{3,2,1,0:T(8,128)} copy(f32[1,1,1024,128]{3,2,1,0:T(8,128)} %shard_map.73) | data formatting | bytes 1048576

commit v2 on v1

--- a/solution.py
+++ b/solution.py
@@ -9,6 +9,8 @@
 LANES = 128
 CHUNK = 128
 INDEX = jnp.int16
+STEPS = 32766.0
+FLOOR = 1e-30
 MESH = pl.DeviceIdType.MESH
 
 
@@ -29,8 +31,8 @@
     def kernel(
         res, inner_inv, inner_idx, dofs, face_inv, face_idx, counts, out,
         inv_in, inv_face, rows, res_t, st_in, st_face, p_t,
-        gathered, pair, joined, terms, back, acc,
-        inv_sem, send_sem, recv_sem, give_sem, back_sem,
+        gathered, pair, joined, kept, terms, peaks, back, back_peaks, acc,
+        inv_sem, send_sem, recv_sem, give_sem, back_sem, peak_sem, back_peak_sem,
     ):
         copies = [pltpu.make_async_copy(inner_inv.at[0, 0], inv_in, inv_sem.at[levels])]
         for k in range(levels):
@@ -82,7 +84,7 @@
         def build_face(k):
             build_stars(st_face.at[k], nint + k * slots, slots, joint)
 
-        send, give = [], []
+        send, give, give_peak = [], [], []
         for k, (target, own, far) in enumerate(places):
             send.append(
                 pltpu.make_async_remote_copy(
@@ -96,10 +98,21 @@
             )
             give.append(
                 pltpu.make_async_remote_copy(
-                    src_ref=terms.at[k, far],
+                    src_ref=terms.at[k],
                     dst_ref=back.at[k],
                     send_sem=give_sem.at[k],
                     recv_sem=back_sem.at[k],
+                    device_id=target,
+                    device_id_type=MESH,
+                )
+            )
+
+            give_peak.append(
+                pltpu.make_async_remote_copy(
+                    src_ref=peaks.at[k],
+                    dst_ref=back_peaks.at[k],
+                    send_sem=peak_sem.at[k],
+                    recv_sem=back_peak_sem.at[k],
                     device_id=target,
                     device_id_type=MESH,
                 )
@@ -148,14 +161,21 @@
                 joined[k, 1], st_face[k, slab:joint, :], preferred_element_type=jnp.float32
             )
             solve(picked, inv_face.at[k], slots)
-            for half in (far, own):
+            def half_terms(half):
                 at = pl.multiple_of(half * slab, slab)
                 both = jnp.dot(
                     st_face[k, pl.ds(at, slab), :],
                     pair[0 : slots * pad],
                     preferred_element_type=jnp.float32,
                 )
-                terms[k, half] = both[:, :nrhs] + both[:, nrhs:]
+                return both[:, :nrhs] + both[:, nrhs:]
+
+            given = half_terms(far)
+            peak = jnp.maximum(jnp.max(jnp.abs(given), axis=0, keepdims=True), FLOOR)
+            peaks[k] = jnp.broadcast_to(peak, peaks.shape[1:])
+            terms[k] = jnp.round(given * (STEPS / peak)).astype(jnp.int32).astype(jnp.int16)
+            kept[k] = half_terms(own)
+            give_peak[k].start()
             give[k].start()
 
         for k in early:
@@ -174,9 +194,11 @@
             face(k)
 
         for k in finish:
-            _, own, _ = places[k]
+            give_peak[k].wait_recv()
             give[k].wait_recv()
-            high, low = split_pair(terms[k, own] + back[k])
+            unit = back_peaks[k, 0:1, :] * (1.0 / STEPS)
+            returned = back[k].astype(jnp.int32).astype(jnp.float32) * unit
+            high, low = split_pair(kept[k] + returned)
             pair[0:slab, 0:nrhs] = high
             pair[0:slab, nrhs : 2 * nrhs] = low
             both = jnp.dot(p_t[k], pair[0:slab], preferred_element_type=jnp.float32)
@@ -188,6 +210,7 @@
         for k in range(levels):
             send[k].wait_send()
             give[k].wait_send()
+            give_peak[k].wait_send()
 
     return kernel
 
@@ -224,10 +247,15 @@
             pltpu.VMEM((nrhs, most), kinds),
             pltpu.VMEM((max(most, slab), 2 * nrhs), kinds),
             pltpu.VMEM((levels, 2, nrhs, slab), kinds),
-            pltpu.VMEM((levels, 2, slab, nrhs), jnp.float32),
             pltpu.VMEM((levels, slab, nrhs), jnp.float32),
+            pltpu.VMEM((levels, slab, nrhs), jnp.int16),
+            pltpu.VMEM((levels, 8, nrhs), jnp.float32),
+            pltpu.VMEM((levels, slab, nrhs), jnp.int16),
+            pltpu.VMEM((levels, 8, nrhs), jnp.float32),
             pltpu.VMEM((ndof, 2 * nrhs), jnp.float32),
             pltpu.SemaphoreType.DMA((levels + 1,)),
+            pltpu.SemaphoreType.DMA((levels,)),
+            pltpu.SemaphoreType.DMA((levels,)),
             pltpu.SemaphoreType.DMA((levels,)),
             pltpu.SemaphoreType.DMA((levels,)),
             pltpu.SemaphoreType.DMA((levels,)),

time: 34.3 us -> 32.3 us (0.942)
  Pallas kernels: 29.9 us -> 27.9 us
    pallas_call x1, Pallas kernels: 29.9 us -> 27.9 us  [on_device(): pl.pallas_call(make_kernel(ndof, nrhs, nint, star, levels, slots, slab, e...]
where the time goes in v2:
time: 32.3 us; the launch traced here: 32.1 us
  Pallas kernels  27.9 us (86%)
  local copies, waits for them, and re-layouts  4.22 us (13%)
    pallas_call x1, Pallas kernels, on_device(): pl.pallas_call(make_kernel(ndof, nrhs, nint, star, levels, slots, slab, e...  27.9 us
    unnamed x2, local copies, waits for them, and re-layouts  4.22 us

profile of v2, /device:TPU:0, one launch (start us, length us, event | category | flops | bytes accessed | tf_op | source)
XLA Modules:
  0.0 32.1 jit_solution(10997331779032679634)
XLA Ops:
  0.0 2.4 %copy.8.inner_inv = bf16[1,1,4,343,343]{4,3,2,1,0:T(8,128)(2,1)} copy(bf16[1,1,4,343,343]{4,2,3,1,0:T(4,128)(2,1)} %param.8) | data formatting | bytes 1882384 | tf_op args[1]
  2.4 27.9 %shard_map.73 = f32[1,1,1024,128]{3,2,1,0:T(8,128)} custom-call(bf16[1,1,1024,128]{3,2,1,0:T(8,128)(2,1)} %res.1, bf16[1,1,4,343,343]{4,3,2,1,0:T(8,128)(2,1)} %copy.8.inner_inv, s32[1,1,4,343]{3,2,1,0:T(4,128)} %inner_idx.1, s32[5,1,512]{2,1,0:T(1,128)} %bitcast.3, bf16[1,1,5,3,343,343]{5,4,3,2,1,0:T(8,128)(2,1)} %face_inv.1, s32[15,1,343]{2,1,0:T(1,128)} %bitcast.2, ...), custom_call_target="tpu_custom_call" | custom-call | tf_op jit(solution)/shard_map/pallas_call | solution.py:234
  30.2 1.9 %copy.10 = f32[1,1,1024,128]{3,2,1,0:T(8,128)} copy(f32[1,1,1024,128]{3,2,1,0:T(8,128)} %shard_map.73) | data formatting | bytes 1048576

commit v3 on v2

--- a/solution.py
+++ b/solution.py
@@ -225,7 +225,7 @@
     pad = round_up(star, LANES)
     joint = 2 * slab
     index_rows = round_up(nint + levels * slots, 8)
-    early, order, finish = (0, 1, 2), (0, 1, 2, 3, 4), (2, 3, 4, 1, 0)
+    early, order, finish = (0, 1), (4, 3, 0, 1, 2), (4, 3, 0, 1, 2)
     kinds = jnp.bfloat16
     vmem = pl.BlockSpec(memory_space=pltpu.VMEM)
     anywhere = pl.BlockSpec(memory_space=pl.ANY)

time: 32.3 us -> 31.1 us (0.963)
  Pallas kernels: 27.9 us -> 26.6 us
    pallas_call x1, Pallas kernels: 27.9 us -> 26.6 us  [on_device(): pl.pallas_call(make_kernel(ndof, nrhs, nint, star, levels, slots, slab, e...]
where the time goes in v3:
time: 31.1 us; the launch traced here: 30.8 us
  Pallas kernels  26.6 us (86%)
  local copies, waits for them, and re-layouts  4.22 us (14%)
    pallas_call x1, Pallas kernels, on_device(): pl.pallas_call(make_kernel(ndof, nrhs, nint, star, levels, slots, slab, e...  26.6 us
    unnamed x2, local copies, waits for them, and re-layouts  4.22 us

profile of v3, /device:TPU:0, one launch (start us, length us, event | category | flops | bytes accessed | tf_op | source)
XLA Modules:
  0.0 30.8 jit_solution(6608332295991750886)
XLA Ops:
  0.0 2.4 %copy.8.inner_inv = bf16[1,1,4,343,343]{4,3,2,1,0:T(8,128)(2,1)} copy(bf16[1,1,4,343,343]{4,2,3,1,0:T(4,128)(2,1)} %param.8) | data formatting | bytes 1882384 | tf_op args[1]
  2.4 26.6 %shard_map.73 = f32[1,1,1024,128]{3,2,1,0:T(8,128)} custom-call(bf16[1,1,1024,128]{3,2,1,0:T(8,128)(2,1)} %res.1, bf16[1,1,4,343,343]{4,3,2,1,0:T(8,128)(2,1)} %copy.8.inner_inv, s32[1,1,4,343]{3,2,1,0:T(4,128)} %inner_idx.1, s32[5,1,512]{2,1,0:T(1,128)} %bitcast.3, bf16[1,1,5,3,343,343]{5,4,3,2,1,0:T(8,128)(2,1)} %face_inv.1, s32[15,1,343]{2,1,0:T(1,128)} %bitcast.2, ...), custom_call_target="tpu_custom_call" | custom-call | tf_op jit(solution)/shard_map/pallas_call | solution.py:234
  29.0 1.9 %copy.10 = f32[1,1,1024,128]{3,2,1,0:T(8,128)} copy(f32[1,1,1024,128]{3,2,1,0:T(8,128)} %shard_map.73) | data formatting | bytes 1048576
